TPU v7x, 32 devices: a whole 2x2x4 slice. The times are simulated.
32 devices in a mesh: items: 8 (over z, y), users: 4 (over x, core).
Axes of the slice: x: 2, y: 2, z: 4, core: 2. Of those that a mesh axis runs over, the one named last changes fastest.
Arguments:
- user_emb: bfloat16 [4096, 256], P('users', 'items'), as said below
- item_emb: bfloat16 [262144, 256], P('items'), as said below
- target: int32 [4096], P('users'), may hold values from 0 to 262143
- history: int32 [4096, 32], P('users'), may hold values from 0 to 262143, as said below
Outputs:
- log_rank: float32 [4096], P('users')
- metrics: float32 [2], replicated
Inputs may be any that keep to these rules, and one draw needn't show every extreme that they name: history[u, k] lies in [k * 8192, (k + 1) * 8192); a user's history entries are thus distinct. `item_emb`: rows of norm about one. `user_emb`: entries of order one.
All inputs are finite; a program needn't handle non-finite values.
Results may differ from a plain program's by a relative error of at most 0.0003.
Values may be sent and summed in bfloat16 or wider, within the bound.
A program may use at most 64 MiB of HBM per device.

v0:
```python
import jax
import jax.numpy as jnp
from jax import lax
from jax.sharding import PartitionSpec as P

sharpness = 4.0


def body(user_emb, item_emb, target, history):
    item_dev = item_emb.shape[0]
    shard = lax.axis_index("items")
    start = shard * item_dev
    local_t = target - start
    inside = (local_t >= 0) & (local_t < item_dev)
    own_rows = item_emb[jnp.clip(local_t, 0, item_dev - 1)]
    users = lax.all_gather(user_emb, "items", axis=1, tiled=True)
    partial_t = jnp.sum(users.astype(jnp.float32) * own_rows.astype(jnp.float32), axis=1)
    tscore = lax.psum(jnp.where(inside, partial_t, 0.0), "items")
    n_items = lax.axis_size("items")
    n_users = lax.axis_size("users")
    u_dev = users.shape[0]
    blk = min(item_dev, 4096)
    nblk = item_dev // blk

    def add_block(index, total):
        rows = lax.dynamic_slice_in_dim(item_emb, index * blk, blk, 0)
        score = lax.dot_general(
            users, rows, (((1,), (1,)), ((), ())), preferred_element_type=jnp.float32
        )
        return total + jnp.sum(jax.nn.sigmoid(sharpness * (score - tscore[:, None])), axis=1)

    total = lax.fori_loop(0, nblk, add_block, jnp.zeros((u_dev,), jnp.float32))
    per_shard = history.shape[1] // n_items
    own_hist = lax.dynamic_slice_in_dim(history, shard * per_shard, per_shard, 1)
    hrows = item_emb[own_hist - start]
    hscore = jnp.einsum("ud,uhd->uh", users, hrows, preferred_element_type=jnp.float32)
    local = total - jnp.sum(jax.nn.sigmoid(sharpness * (hscore - tscore[:, None])), axis=1)
    seen = jnp.any(history == target[:, None], axis=1)
    correction = jnp.where(seen, 0.0, 0.5).astype(jnp.float32)
    all_users = u_dev * n_users
    above = lax.psum(local, "items") - correction
    rank = 1.0 + above
    log_rank = jnp.log(rank)
    hit = jax.nn.sigmoid(10.5 - rank)
    gain = hit / jnp.log2(1.0 + rank)
    hit_sum, gain_sum = lax.psum((jnp.sum(hit), jnp.sum(gain)), "users")
    metrics = jnp.stack([hit_sum, gain_sum]) / all_users
    return (log_rank, metrics)


def solution(mesh):
    return jax.shard_map(
        body,
        mesh=mesh,
        in_specs=(P("users", "items"), P("items", None), P("users"), P("users", None)),
        out_specs=(P("users"), P()),
        check_vma=False,
    )
```

profile of v0, /device:TPU:0, one launch (start us, length us, event | category | flops | bytes accessed | tf_op | source)
XLA Modules:
  0.0 174.1 jit_solution(5118468006411309888)
XLA Ops:
  0.6 0.0 copy-start.1
  0.6 0.0 copy-start.2
  0.7 0.8 compare_select_fusion
  1.5 0.2 copy.14
  1.7 0.3 reshape.17
  2.0 20.9 %gather_fusion.1 = bf16[4096,256]{1,0:T(8,128)(2,1)S(1)} fusion(bf16[32768,256]{1,0:T(8,128)(2,1)} %param.7, s32[4096]{0:T(1024)S(1)} %broadcast_clamp_fusion), kind=kCustom, calls=%fused_computation.1 | custom fusion | bytes 4210688 | tf_op jit(solution)/shard_map/gather | solution.py:35
  22.9 2.1 %reshape.16 = bf16[1024,4,256]{2,1,0:T(4,128)(2,1)} reshape(bf16[4096,256]{1,0:T(8,128)(2,1)S(1)} %gather_fusion.1) | data formatting | bytes 4194304 | tf_op jit(solution)/shard_map/gather | solution.py:35
  25.0 0.0 copy-done.1
  25.0 33.0 %all_gather.3 = bf16[1024,256]{0,1:T(8,128)(2,1)S(1)} all-gather(bf16[1024,32]{0,1:T(8,128)(2,1)S(1)} %copy-done.1), channel_id=1, replica_groups=mesh['items'=8,'users'=4] {'items'}, dimensions={1}, use_global_device_ids=true | all-gather | bytes 589824 | tf_op jit(solution)/shard_map/all_gather | solution.py:16
  58.0 0.2 copy.20
  58.2 2.9 %multiply_reduce_fusion = f32[1024,4]{1,0:T(8,128)S(1)} fusion(f32[1024,256]{1,0:T(8,128)S(1)} %copy.20, bf16[1024,4,256]{2,1,0:T(4,128)(2,1)} %reshape.16), kind=kLoop, calls=%fused_computation.7 | loop fusion | flops 3141632 | bytes 3162112
  61.1 0.2 copy.19
  61.3 0.0 copy-done.2
  61.3 11.4 %gather_fusion = bf16[1024,256]{1,0:T(8,128)(2,1)S(1)} fusion(bf16[32768,256]{1,0:T(8,128)(2,1)} %param.7, s32[1024]{0:T(1024)S(1)} %fusion.4), kind=kCustom, calls=%fused_computation | custom fusion | bytes 1052672 | tf_op jit(solution)/shard_map/gather | solution.py:15
  72.7 0.2 copy.13
  73.0 0.2 multiply_reduce_fusion.1
  73.2 21.5 %psum.28 = f32[1024]{0:T(1024)S(1)} all-reduce(f32[1024]{0:T(1024)S(1)} %and_select_fusion), channel_id=1, replica_groups=mesh['items'=8,'users'=4] {'items'}, use_global_device_ids=true, to_apply=%region_1.2 | all-reduce | flops 1024 | bytes 8192 | tf_op jit(solution)/shard_map/psum | solution.py:18
  94.8 0.0 copy-start
  94.8 52.7 %while.14 = (s32[]{:T(128)}, f32[1024]{0:T(1024)S(1)}, bf16[32768,256]{1,0:T(8,128)(2,1)}, bf16[1024,256]{1,0:T(8,128)(2,1)S(1)}, f32[1024]{0:T(1024)S(1)}, /*index=5*/s32[]{:T(128)}, s32[]{:T(128)}, s32[]{:T(128)}, s32[]{:T(128)}) while((s32[]{:T(128)}, f32[1024]{0:T(1024)S(1)}, bf16[32768,256]{1,0:T(8,128)(2,1)}, ...), condition=%wide.region_4.5_spmd.clone, body=%wide.region_2.4_spmd.clone.sunk | while | flops 2172650496 | bytes 2642073 | solution.py:32
  94.8 6.6 %fusion.11 = f32[1024]{0:T(1024)S(1)} fusion(bf16[1024,256]{1,0:T(8,128)(2,1)S(1)} %get-tuple-element.192, f32[1024]{0:T(1024)S(1)} %get-tuple-element.193, bf16[32768,256]{1,0:T(8,128)(2,1)} %get-tuple-element.191, s32[]{:T(128)S(6)} %select_n.43), kind=kOutput, calls=%fused_computation.3.clone.1 | convolution fusion | flops 2172648448 | bytes 2629636 | tf_op jit(solution)/shard_map/while/body/eval_jaxpr/dot_general | solution.py:27
  101.4 6.5 %fusion.11 = f32[1024]{0:T(1024)S(1)} fusion(bf16[1024,256]{1,0:T(8,128)(2,1)S(1)} %get-tuple-element.192, f32[1024]{0:T(1024)S(1)} %get-tuple-element.193, bf16[32768,256]{1,0:T(8,128)(2,1)} %get-tuple-element.191, s32[]{:T(128)S(6)} %select_n.43), kind=kOutput, calls=%fused_computation.3.clone.1 | convolution fusion | flops 2172648448 | bytes 2629636 | tf_op jit(solution)/shard_map/while/body/eval_jaxpr/dot_general | solution.py:27
  108.0 6.5 %fusion.11 = f32[1024]{0:T(1024)S(1)} fusion(bf16[1024,256]{1,0:T(8,128)(2,1)S(1)} %get-tuple-element.192, f32[1024]{0:T(1024)S(1)} %get-tuple-element.193, bf16[32768,256]{1,0:T(8,128)(2,1)} %get-tuple-element.191, s32[]{:T(128)S(6)} %select_n.43), kind=kOutput, calls=%fused_computation.3.clone.1 | convolution fusion | flops 2172648448 | bytes 2629636 | tf_op jit(solution)/shard_map/while/body/eval_jaxpr/dot_general | solution.py:27
  114.6 6.5 %fusion.11 = f32[1024]{0:T(1024)S(1)} fusion(bf16[1024,256]{1,0:T(8,128)(2,1)S(1)} %get-tuple-element.192, f32[1024]{0:T(1024)S(1)} %get-tuple-element.193, bf16[32768,256]{1,0:T(8,128)(2,1)} %get-tuple-element.191, s32[]{:T(128)S(6)} %select_n.43), kind=kOutput, calls=%fused_computation.3.clone.1 | convolution fusion | flops 2172648448 | bytes 2629636 | tf_op jit(solution)/shard_map/while/body/eval_jaxpr/dot_general | solution.py:27
  121.2 6.5 %fusion.11 = f32[1024]{0:T(1024)S(1)} fusion(bf16[1024,256]{1,0:T(8,128)(2,1)S(1)} %get-tuple-element.192, f32[1024]{0:T(1024)S(1)} %get-tuple-element.193, bf16[32768,256]{1,0:T(8,128)(2,1)} %get-tuple-element.191, s32[]{:T(128)S(6)} %select_n.43), kind=kOutput, calls=%fused_computation.3.clone.1 | convolution fusion | flops 2172648448 | bytes 2629636 | tf_op jit(solution)/shard_map/while/body/eval_jaxpr/dot_general | solution.py:27
  127.8 6.5 %fusion.11 = f32[1024]{0:T(1024)S(1)} fusion(bf16[1024,256]{1,0:T(8,128)(2,1)S(1)} %get-tuple-element.192, f32[1024]{0:T(1024)S(1)} %get-tuple-element.193, bf16[32768,256]{1,0:T(8,128)(2,1)} %get-tuple-element.191, s32[]{:T(128)S(6)} %select_n.43), kind=kOutput, calls=%fused_computation.3.clone.1 | convolution fusion | flops 2172648448 | bytes 2629636 | tf_op jit(solution)/shard_map/while/body/eval_jaxpr/dot_general | solution.py:27
  134.4 6.5 %fusion.11 = f32[1024]{0:T(1024)S(1)} fusion(bf16[1024,256]{1,0:T(8,128)(2,1)S(1)} %get-tuple-element.192, f32[1024]{0:T(1024)S(1)} %get-tuple-element.193, bf16[32768,256]{1,0:T(8,128)(2,1)} %get-tuple-element.191, s32[]{:T(128)S(6)} %select_n.43), kind=kOutput, calls=%fused_computation.3.clone.1 | convolution fusion | flops 2172648448 | bytes 2629636 | tf_op jit(solution)/shard_map/while/body/eval_jaxpr/dot_general | solution.py:27
  140.9 6.5 %fusion.11 = f32[1024]{0:T(1024)S(1)} fusion(bf16[1024,256]{1,0:T(8,128)(2,1)S(1)} %get-tuple-element.192, f32[1024]{0:T(1024)S(1)} %get-tuple-element.193, bf16[32768,256]{1,0:T(8,128)(2,1)} %get-tuple-element.191, s32[]{:T(128)S(6)} %select_n.43), kind=kOutput, calls=%fused_computation.3.clone.1 | convolution fusion | flops 2172648448 | bytes 2629636 | tf_op jit(solution)/shard_map/while/body/eval_jaxpr/dot_general | solution.py:27
  147.5 17.1 %psum.29 = f32[1024]{0:T(1024)S(1)} all-reduce(f32[1024]{0:T(1024)S(1)} %sub.59), channel_id=1, replica_groups=mesh['items'=8,'users'=4] {'items'}, use_global_device_ids=true, to_apply=%region_6.7 | all-reduce | flops 1024 | bytes 8192 | tf_op jit(solution)/shard_map/psum | solution.py:41
  164.7 0.0 copy-done
  164.7 1.3 divide_reduce_fusion.1
  166.0 6.3 %all-reduce = (f32[1]{0:T(128)}, f32[1]{0:T(128)}) all-reduce(f32[1]{0:T(128)} %bitcast.2, f32[1]{0:T(128)} %bitcast.1), channel_id=1, replica_groups=mesh['items'=8,'users'=4] {'users'}, use_global_device_ids=true, to_apply=%region_11.12 | all-reduce | flops 2 | bytes 16 | tf_op jit(solution)/shard_map/psum | solution.py:46
  172.3 1.8 %maximum_multiply_fusion = f32[2]{0:T(128)} fusion(f32[1]{0:T(128)} %get-tuple-element.137, f32[1]{0:T(128)} %get-tuple-element.138), kind=kLoop, calls=%fused_computation.22 | loop fusion | flops 4 | bytes 16 | tf_op jit(solution)/shard_map/div | solution.py:47
  (15 shorter events, 0.1 us)
Async XLA Ops:
  0.6 24.4 %copy-start.1 = (bf16[1024,32]{0,1:T(8,128)(2,1)S(1)}, bf16[1024,32]{0,1:T(8,128)(2,1)}, u32[]{:S(2)}) copy-start(bf16[1024,32]{0,1:T(8,128)(2,1)} %param.6) | copy-start | bytes 196612
  0.6 60.7 %copy-start.2 = (s32[1024]{0:T(1024)S(1)}, s32[1024]{0:T(1024)}, u32[]{:S(2)}) copy-start(s32[1024]{0:T(1024)} %param.8) | copy-start | bytes 12292
  94.8 69.9 %copy-start = (s32[1024,32]{0,1:T(8,128)S(1)}, s32[1024,32]{0,1:T(8,128)}, u32[]{:S(2)}) copy-start(s32[1024,32]{0,1:T(8,128)} %param.9) | copy-start | bytes 393220
where the time goes:
time: 175 us; the launch traced here: 174 us
  blocking collectives  78 us (45%)
  matrix products  52.4 us (30%)
  local copies, waits for them, and re-layouts  35.5 us (20%)
  other arithmetic  7.14 us (4%)
    dot_general x8, matrix products, add_block(): lax.dot_general(users, rows, (((1,), (1,)), ((), ())), preferred_element_...  52.4 us
    all_gather x1, blocking collectives, body(): users = lax.all_gather(user_emb, 'items', axis=1, tiled=True)  33 us
    gather x2, local copies, waits for them, and re-layouts, body(): hrows = item_emb[own_hist - start]  23 us
    psum x1, blocking collectives, body(): tscore = lax.psum(jnp.where(inside, partial_t, 0.0), 'items')  21.5 us
    psum x1, blocking collectives, body(): above = lax.psum(local, 'items') - correction  17.1 us
    gather x1, local copies, waits for them, and re-layouts, body(): own_rows = item_emb[jnp.clip(local_t, 0, item_dev - 1)]  11.4 us
    psum x1, blocking collectives, body(): hit_sum, gain_sum = lax.psum((jnp.sum(hit), jnp.sum(gain)), 'users')  6.3 us

commit v1 on v0

--- a/solution.py
+++ b/solution.py
@@ -13,7 +13,14 @@
     local_t = target - start
     inside = (local_t >= 0) & (local_t < item_dev)
     own_rows = item_emb[jnp.clip(local_t, 0, item_dev - 1)]
-    users = lax.all_gather(user_emb, "items", axis=1, tiled=True)
+    ring = [user_emb]
+    for hop in range(7):
+        ring.append(lax.ppermute(ring[-1], "items", [(dev, (dev + 1) % 8) for dev in range(8)]))
+    users = jnp.roll(
+        jnp.concatenate(ring[::-1], axis=1),
+        (lax.axis_index("items") + 1) * ring[0].shape[1],
+        axis=1,
+    )
     partial_t = jnp.sum(users.astype(jnp.float32) * own_rows.astype(jnp.float32), axis=1)
     tscore = lax.psum(jnp.where(inside, partial_t, 0.0), "items")
     n_items = lax.axis_size("items")

time: 175 us -> 211 us (1.21)
  waiting for transfers between devices: 0 us -> 54.6 us
  blocking collectives: 78 us -> 42.6 us
  local copies, waits for them, and re-layouts: 35.5 us -> 46 us
  starting transfers between devices: 0 us -> 3.06 us
  matrix products: 52.4 us -> 55.1 us
    ppermute x0 -> x7, waiting for transfers between devices: none -> 54.6 us  [body(): lax.ppermute(ring[-1], 'items', [(dev, (dev + 1) % 8) for dev in range(8)])]
    all_gather x1 -> x0, blocking collectives: 33 us -> none  [body(): users = lax.all_gather(user_emb, 'items', axis=1, tiled=True)]
    concatenate x0 -> x1, local copies, waits for them, and re-layouts: none -> 5.06 us  [body(): jnp.roll(jnp.concatenate(ring[::-1], axis=1), (lax.axis_index('items') +...]
    while x0 -> x32, local copies, waits for them, and re-layouts: none -> 4.7 us
    ppermute x0 -> x7, starting transfers between devices: none -> 3.06 us  [body(): lax.ppermute(ring[-1], 'items', [(dev, (dev + 1) % 8) for dev in range(8)])]
    unnamed x2 -> x1, other arithmetic: 2.91 us -> 0.01 us
    dot_general x0 -> x1, matrix products: none -> 2.81 us  [body(): jnp.einsum('ud,uhd->uh', users, hrows, preferred_element_type=jnp.float32)]
    psum x1, blocking collectives: 21.5 us -> 19.2 us  [body(): tscore = lax.psum(jnp.where(inside, partial_t, 0.0), 'items')]
  transfers between devices with their start and end apart: 0 -> 7, of which waited for: 0 -> 6; matrix products, arithmetic and copies ran while one was open for 0% -> 18% of each run, Pallas kernels for 0% -> 0%
where the time goes in v1:
time: 211 us; the launch traced here: 210 us
  matrix products  55.1 us (26%)
  waiting for transfers between devices  54.6 us (26%)
  local copies, waits for them, and re-layouts  46 us (22%)
  blocking collectives  42.6 us (20%)
  other arithmetic  7.4 us (4%)
  starting transfers between devices  3.06 us (1%)
    ppermute x7, waiting for transfers between devices, body(): lax.ppermute(ring[-1], 'items', [(dev, (dev + 1) % 8) for dev in range(8)])  54.6 us
    dot_general x8, matrix products, add_block(): lax.dot_general(users, rows, (((1,), (1,)), ((), ())), preferred_element_...  52.3 us
    gather x2, local copies, waits for them, and re-layouts, body(): hrows = item_emb[own_hist - start]  23 us
    psum x1, blocking collectives, body(): tscore = lax.psum(jnp.where(inside, partial_t, 0.0), 'items')  19.2 us
    psum x1, blocking collectives, body(): above = lax.psum(local, 'items') - correction  17.1 us
    gather x1, local copies, waits for them, and re-layouts, body(): own_rows = item_emb[jnp.clip(local_t, 0, item_dev - 1)]  11.4 us
    psum x1, blocking collectives, body(): hit_sum, gain_sum = lax.psum((jnp.sum(hit), jnp.sum(gain)), 'users')  6.3 us
    concatenate x1, local copies, waits for them, and re-layouts, body(): jnp.roll(jnp.concatenate(ring[::-1], axis=1), (lax.axis_index('items') +...  5.06 us
  transfers between devices with their start and end apart: 7, of which 6 were waited for; matrix products, arithmetic and copies ran while one was open for 18% of the time, Pallas kernels for 0%

profile of v1, /device:TPU:0, one launch (start us, length us, event | category | flops | bytes accessed | tf_op | source)
XLA Modules:
  0.0 209.8 jit_solution(5084373364069518410)
XLA Ops:
  0.6 1.0 copy.13
  1.7 3.0 %collective-permute-start = (bf16[1024,32]{1,0:T(8,128)(2,1)S(1)}, bf16[1024,32]{1,0:T(8,128)(2,1)S(1)}, u32[]{:S(2)}, u32[]{:S(2)}) collective-permute-start(bf16[1024,32]{1,0:T(8,128)(2,1)S(1)} %copy.13), channel_id=1, source_target_pairs={{0,4},{4,8},{8,12},{12,16},{16,20},{20,24},{24,28},{28,0},{1,5},{5... | collective-permute-start | bytes 196616 | tf_op jit(solution)/shard_map/ppermute | solution.py:18
  4.7 9.3 %collective-permute-done = bf16[1024,32]{1,0:T(8,128)(2,1)S(1)} collective-permute-done((bf16[1024,32]{1,0:T(8,128)(2,1)S(1)}, bf16[1024,32]{1,0:T(8,128)(2,1)S(1)}, u32[]{:S(2)}, u32[]{:S(2)}) %collective-permute-start) | collective-permute-done | bytes 65568 | tf_op jit(solution)/shard_map/ppermute | solution.py:18
  14.1 10.2 %collective-permute-done.1 = bf16[1024,32]{1,0:T(8,128)(2,1)S(1)} collective-permute-done((bf16[1024,32]{1,0:T(8,128)(2,1)S(1)}, bf16[1024,32]{1,0:T(8,128)(2,1)S(1)}, u32[]{:S(2)}, u32[]{:S(2)}) %collective-permute-start.1) | collective-permute-done | bytes 65568 | tf_op jit(solution)/shard_map/ppermute | solution.py:18
  24.3 9.3 %collective-permute-done.2 = bf16[1024,32]{1,0:T(8,128)(2,1)S(1)} collective-permute-done((bf16[1024,32]{1,0:T(8,128)(2,1)S(1)}, bf16[1024,32]{1,0:T(8,128)(2,1)S(1)}, u32[]{:S(2)}, u32[]{:S(2)}) %collective-permute-start.2) | collective-permute-done | bytes 65568 | tf_op jit(solution)/shard_map/ppermute | solution.py:18
  33.6 0.8 compare_select_fusion
  34.4 0.2 copy.16
  34.6 0.3 reshape.17
  34.9 7.9 %collective-permute-done.3 = bf16[1024,32]{1,0:T(8,128)(2,1)} collective-permute-done((bf16[1024,32]{1,0:T(8,128)(2,1)S(1)}, bf16[1024,32]{1,0:T(8,128)(2,1)}, u32[]{:S(2)}, u32[]{:S(2)}) %collective-permute-start.3) | collective-permute-done | bytes 65568 | tf_op jit(solution)/shard_map/ppermute | solution.py:18
  42.7 9.4 %collective-permute-done.4 = bf16[1024,32]{1,0:T(8,128)(2,1)} collective-permute-done((bf16[1024,32]{1,0:T(8,128)(2,1)}, bf16[1024,32]{1,0:T(8,128)(2,1)}, u32[]{:S(2)}, u32[]{:S(2)}) %collective-permute-start.4) | collective-permute-done | bytes 65568 | tf_op jit(solution)/shard_map/ppermute | solution.py:18
  52.1 0.7 fusion.11
  52.8 11.4 %gather_fusion = bf16[1024,256]{1,0:T(8,128)(2,1)S(1)} fusion(bf16[32768,256]{1,0:T(8,128)(2,1)} %param.7, s32[1024]{0:T(1024)S(1)} %fusion.11), kind=kCustom, calls=%fused_computation | custom fusion | bytes 1052672 | tf_op jit(solution)/shard_map/gather | solution.py:15
  64.2 20.9 %gather_fusion.1 = bf16[4096,256]{1,0:T(8,128)(2,1)S(1)} fusion(bf16[32768,256]{1,0:T(8,128)(2,1)} %param.7, s32[4096]{0:T(1024)S(1)} %broadcast_clamp_fusion), kind=kCustom, calls=%fused_computation.1 | custom fusion | bytes 4210688 | tf_op jit(solution)/shard_map/gather | solution.py:42
  85.2 2.1 reshape.16
  87.3 0.7 compare_reduce_fusion
  88.0 8.6 %collective-permute-done.6 = bf16[1024,32]{1,0:T(8,128)(2,1)S(1)} collective-permute-done((bf16[1024,32]{1,0:T(8,128)(2,1)}, bf16[1024,32]{1,0:T(8,128)(2,1)S(1)}, u32[]{:S(2)}, u32[]{:S(2)}) %collective-permute-start.6) | collective-permute-done | bytes 65568 | tf_op jit(solution)/shard_map/ppermute | solution.py:18
  96.5 5.1 %concatenate.6 = bf16[1024,512]{1,0:T(8,128)(2,1)S(1)} concatenate(bf16[1024,32]{1,0:T(8,128)(2,1)S(1)} %collective-permute-done.6, bf16[1024,32]{1,0:T(8,128)(2,1)} %collective-permute-done.5, bf16[1024,32]{1,0:T(8,128)(2,1)} %collective-permute-done.4, bf16[1024,32]{1,0:T(8,128)(2,1)} %collective-permute-done.3, bf16[1024,32]{1,0:T(8,128)(2,1)} %copy-done, ...), dimensions={1} | concatenate | bytes 2097152 | tf_op jit(solution)/shard_map/jit(_roll_dynamic)/concatenate | solution.py:19
  101.6 0.7 multiply_reduce_fusion
  102.2 2.8 %fusion.3 = f32[1024,1,4]{2,1,0:T(1,128)S(1)} fusion(bf16[1024,4,256]{2,1,0:T(4,128)(2,1)} %reshape.16, bf16[1024,256,1]{1,0,2:T(8,128)(2,1)S(1)} %bitcast.21), kind=kOutput, calls=%fused_computation.8 | convolution fusion | flops 2097152 | bytes 2637824 | tf_op jit(solution)/shard_map/ud,uhd->uh/dot_general | solution.py:43
  105.1 0.3 copy.18
  105.3 0.7 and_select_fusion
  106.1 19.2 %psum.28 = f32[1024]{0:T(1024)S(1)} all-reduce(f32[1024]{0:T(1024)S(1)} %and_select_fusion), channel_id=1, replica_groups=mesh['items'=8,'users'=4] {'items'}, use_global_device_ids=true, to_apply=%region_1.2 | all-reduce | flops 1024 | bytes 8192 | tf_op jit(solution)/shard_map/psum | solution.py:25
  125.2 57.4 %while.14 = (s32[]{:T(128)}, f32[1024]{0:T(1024)}, bf16[32768,256]{1,0:T(8,128)(2,1)}, bf16[1024,256]{1,0:T(8,128)(2,1)S(1)}, f32[1024]{0:T(1024)S(1)}, /*index=5*/s32[]{:T(128)}, s32[]{:T(128)}, s32[]{:T(128)}, s32[]{:T(128)}) while((s32[]{:T(128)}, f32[1024]{0:T(1024)}, bf16[32768,256]{1,0:T(8,128)(2,1)}, ...), condition=%wide.region_4.5_spmd.clone, body=%wide.region_2.4_spmd.clone.sunk | while | flops 2172650496 | bytes 2674897 | solution.py:39
  125.3 6.5 %fusion.19 = f32[1024]{0:T(1024)S(1)} fusion(bf16[1024,256]{1,0:T(8,128)(2,1)S(1)} %get-tuple-element.184, f32[1024]{0:T(1024)S(1)} %get-tuple-element.185, bf16[32768,256]{1,0:T(8,128)(2,1)} %get-tuple-element.183, s32[]{:T(128)S(6)} %select_n.58), kind=kOutput, calls=%fused_computation.3.clone.1 | convolution fusion | flops 2172648448 | bytes 2629636 | tf_op jit(solution)/shard_map/while/body/eval_jaxpr/dot_general | solution.py:34
  131.9 0.6 copy-done.3
  132.5 6.5 %fusion.19 = f32[1024]{0:T(1024)S(1)} fusion(bf16[1024,256]{1,0:T(8,128)(2,1)S(1)} %get-tuple-element.184, f32[1024]{0:T(1024)S(1)} %get-tuple-element.185, bf16[32768,256]{1,0:T(8,128)(2,1)} %get-tuple-element.183, s32[]{:T(128)S(6)} %select_n.58), kind=kOutput, calls=%fused_computation.3.clone.1 | convolution fusion | flops 2172648448 | bytes 2629636 | tf_op jit(solution)/shard_map/while/body/eval_jaxpr/dot_general | solution.py:34
  139.0 0.6 copy-done.3
  139.6 6.5 %fusion.19 = f32[1024]{0:T(1024)S(1)} fusion(bf16[1024,256]{1,0:T(8,128)(2,1)S(1)} %get-tuple-element.184, f32[1024]{0:T(1024)S(1)} %get-tuple-element.185, bf16[32768,256]{1,0:T(8,128)(2,1)} %get-tuple-element.183, s32[]{:T(128)S(6)} %select_n.58), kind=kOutput, calls=%fused_computation.3.clone.1 | convolution fusion | flops 2172648448 | bytes 2629636 | tf_op jit(solution)/shard_map/while/body/eval_jaxpr/dot_general | solution.py:34
  146.2 0.0 copy-start.3
  146.2 0.6 copy-done.3
  146.8 6.5 %fusion.19 = f32[1024]{0:T(1024)S(1)} fusion(bf16[1024,256]{1,0:T(8,128)(2,1)S(1)} %get-tuple-element.184, f32[1024]{0:T(1024)S(1)} %get-tuple-element.185, bf16[32768,256]{1,0:T(8,128)(2,1)} %get-tuple-element.183, s32[]{:T(128)S(6)} %select_n.58), kind=kOutput, calls=%fused_computation.3.clone.1 | convolution fusion | flops 2172648448 | bytes 2629636 | tf_op jit(solution)/shard_map/while/body/eval_jaxpr/dot_general | solution.py:34
  153.4 0.0 copy-start.3
  153.4 0.6 copy-done.3
  154.0 6.5 %fusion.19 = f32[1024]{0:T(1024)S(1)} fusion(bf16[1024,256]{1,0:T(8,128)(2,1)S(1)} %get-tuple-element.184, f32[1024]{0:T(1024)S(1)} %get-tuple-element.185, bf16[32768,256]{1,0:T(8,128)(2,1)} %get-tuple-element.183, s32[]{:T(128)S(6)} %select_n.58), kind=kOutput, calls=%fused_computation.3.clone.1 | convolution fusion | flops 2172648448 | bytes 2629636 | tf_op jit(solution)/shard_map/while/body/eval_jaxpr/dot_general | solution.py:34
  160.5 0.0 copy-start.3
  160.5 0.6 copy-done.3
  161.1 6.5 %fusion.19 = f32[1024]{0:T(1024)S(1)} fusion(bf16[1024,256]{1,0:T(8,128)(2,1)S(1)} %get-tuple-element.184, f32[1024]{0:T(1024)S(1)} %get-tuple-element.185, bf16[32768,256]{1,0:T(8,128)(2,1)} %get-tuple-element.183, s32[]{:T(128)S(6)} %select_n.58), kind=kOutput, calls=%fused_computation.3.clone.1 | convolution fusion | flops 2172648448 | bytes 2629636 | tf_op jit(solution)/shard_map/while/body/eval_jaxpr/dot_general | solution.py:34
  167.7 0.6 copy-done.3
  168.3 6.5 %fusion.19 = f32[1024]{0:T(1024)S(1)} fusion(bf16[1024,256]{1,0:T(8,128)(2,1)S(1)} %get-tuple-element.184, f32[1024]{0:T(1024)S(1)} %get-tuple-element.185, bf16[32768,256]{1,0:T(8,128)(2,1)} %get-tuple-element.183, s32[]{:T(128)S(6)} %select_n.58), kind=kOutput, calls=%fused_computation.3.clone.1 | convolution fusion | flops 2172648448 | bytes 2629636 | tf_op jit(solution)/shard_map/while/body/eval_jaxpr/dot_general | solution.py:34
  174.9 0.6 copy-done.3
  175.5 6.5 %fusion.19 = f32[1024]{0:T(1024)S(1)} fusion(bf16[1024,256]{1,0:T(8,128)(2,1)S(1)} %get-tuple-element.184, f32[1024]{0:T(1024)S(1)} %get-tuple-element.185, bf16[32768,256]{1,0:T(8,128)(2,1)} %get-tuple-element.183, s32[]{:T(128)S(6)} %select_n.58), kind=kOutput, calls=%fused_computation.3.clone.1 | convolution fusion | flops 2172648448 | bytes 2629636 | tf_op jit(solution)/shard_map/while/body/eval_jaxpr/dot_general | solution.py:34
  182.0 0.0 copy-start.3
  182.0 0.6 copy-done.3
  182.6 0.7 sub.64
  183.3 17.1 %psum.29 = f32[1024]{0:T(1024)S(1)} all-reduce(f32[1024]{0:T(1024)S(1)} %sub.64), channel_id=1, replica_groups=mesh['items'=8,'users'=4] {'items'}, use_global_device_ids=true, to_apply=%region_6.7 | all-reduce | flops 1024 | bytes 8192 | tf_op jit(solution)/shard_map/psum | solution.py:48
  200.4 1.3 divide_reduce_fusion.1
  201.7 6.3 %all-reduce = (f32[1]{0:T(128)}, f32[1]{0:T(128)}) all-reduce(f32[1]{0:T(128)} %bitcast.3, f32[1]{0:T(128)} %bitcast.2), channel_id=1, replica_groups=mesh['items'=8,'users'=4] {'users'}, use_global_device_ids=true, to_apply=%region_11.12 | all-reduce | flops 2 | bytes 16 | tf_op jit(solution)/shard_map/psum | solution.py:53
  208.0 1.8 maximum_multiply_fusion
  (42 shorter events, 0.2 us)
Async XLA Ops:
  0.6 86.6 %copy-start.1 = (s32[1024,32]{0,1:T(8,128)S(1)}, s32[1024,32]{0,1:T(8,128)}, u32[]{:S(2)}) copy-start(s32[1024,32]{0,1:T(8,128)} %param.9) | copy-start | bytes 393220
  1.7 12.4 %collective-permute-start = (bf16[1024,32]{1,0:T(8,128)(2,1)S(1)}, bf16[1024,32]{1,0:T(8,128)(2,1)S(1)}, u32[]{:S(2)}, u32[]{:S(2)}) collective-permute-start(bf16[1024,32]{1,0:T(8,128)(2,1)S(1)} %copy.13), channel_id=1, source_target_pairs={{0,4},{4,8},{8,12},{12,16},{16,20},{20,24},{24,28},{28,0},{1,5},{5... | collective-permute-start | bytes 196616 | tf_op jit(solution)/shard_map/ppermute | solution.py:18
  14.1 10.2 %collective-permute-start.1 = (bf16[1024,32]{1,0:T(8,128)(2,1)S(1)}, bf16[1024,32]{1,0:T(8,128)(2,1)S(1)}, u32[]{:S(2)}, u32[]{:S(2)}) collective-permute-start(bf16[1024,32]{1,0:T(8,128)(2,1)S(1)} %collective-permute-done), channel_id=1, source_target_pairs={{0,4},{4,8},{8,12},{12,16},{16,20},{20,24},{24,28},{28,0},{1,5},{5... | collective-permute-start | bytes 196616 | tf_op jit(solution)/shard_map/ppermute | solution.py:18
  24.2 9.3 %collective-permute-start.2 = (bf16[1024,32]{1,0:T(8,128)(2,1)S(1)}, bf16[1024,32]{1,0:T(8,128)(2,1)S(1)}, u32[]{:S(2)}, u32[]{:S(2)}) collective-permute-start(bf16[1024,32]{1,0:T(8,128)(2,1)S(1)} %collective-permute-done.1), channel_id=1, source_target_pairs={{0,4},{4,8},{8,12},{12,16},{16,20},{20,24},{24,28},{28,0},{1,5},{5... | collective-permute-start | bytes 196616 | tf_op jit(solution)/shard_map/ppermute | solution.py:18
  33.6 19.3 %copy-start = (bf16[1024,32]{1,0:T(8,128)(2,1)}, bf16[1024,32]{1,0:T(8,128)(2,1)S(1)}, u32[]{:S(2)}) copy-start(bf16[1024,32]{1,0:T(8,128)(2,1)S(1)} %collective-permute-done.2) | copy-start | bytes 196612
  33.6 9.2 %collective-permute-start.3 = (bf16[1024,32]{1,0:T(8,128)(2,1)S(1)}, bf16[1024,32]{1,0:T(8,128)(2,1)}, u32[]{:S(2)}, u32[]{:S(2)}) collective-permute-start(bf16[1024,32]{1,0:T(8,128)(2,1)S(1)} %collective-permute-done.2), channel_id=1, source_target_pairs={{0,4},{4,8},{8,12},{12,16},{16,20},{20,24},{24,28},{28,0},{1,5},{5... | collective-permute-start | bytes 196616 | tf_op jit(solution)/shard_map/ppermute | solution.py:18
  42.7 9.4 %collective-permute-start.4 = (bf16[1024,32]{1,0:T(8,128)(2,1)}, bf16[1024,32]{1,0:T(8,128)(2,1)}, u32[]{:S(2)}, u32[]{:S(2)}) collective-permute-start(bf16[1024,32]{1,0:T(8,128)(2,1)} %collective-permute-done.3), channel_id=1, source_target_pairs={{0,4},{4,8},{8,12},{12,16},{16,20},{20,24},{24,28},{28,0},{1,5},{5... | collective-permute-start | bytes 196616 | tf_op jit(solution)/shard_map/ppermute | solution.py:18
  52.1 35.1 %collective-permute-start.5 = (bf16[1024,32]{1,0:T(8,128)(2,1)}, bf16[1024,32]{1,0:T(8,128)(2,1)}, u32[]{:S(2)}, u32[]{:S(2)}) collective-permute-start(bf16[1024,32]{1,0:T(8,128)(2,1)} %collective-permute-done.4), channel_id=1, source_target_pairs={{0,4},{4,8},{8,12},{12,16},{16,20},{20,24},{24,28},{28,0},{1,5},{5... | collective-permute-start | bytes 196616 | tf_op jit(solution)/shard_map/ppermute | solution.py:18
  87.2 9.3 %collective-permute-start.6 = (bf16[1024,32]{1,0:T(8,128)(2,1)}, bf16[1024,32]{1,0:T(8,128)(2,1)S(1)}, u32[]{:S(2)}, u32[]{:S(2)}) collective-permute-start(bf16[1024,32]{1,0:T(8,128)(2,1)} %collective-permute-done.5), channel_id=1, source_target_pairs={{0,4},{4,8},{8,12},{12,16},{16,20},{20,24},{24,28},{28,0},{1,5},{5... | collective-permute-start | bytes 196616 | tf_op jit(solution)/shard_map/ppermute | solution.py:18
  125.3 6.6 %copy-start.2 = (f32[1024]{0:T(1024)S(1)}, f32[1024]{0:T(1024)}, u32[]{:S(2)}) copy-start(f32[1024]{0:T(1024)} %get-tuple-element.173) | copy-start | bytes 12292 | tf_op jit(solution)/shard_map/while
  131.9 0.6 copy-start.3
  132.5 6.5 %copy-start.2 = (f32[1024]{0:T(1024)S(1)}, f32[1024]{0:T(1024)}, u32[]{:S(2)}) copy-start(f32[1024]{0:T(1024)} %get-tuple-element.173) | copy-start | bytes 12292 | tf_op jit(solution)/shard_map/while
  139.0 0.6 copy-start.3
  139.6 6.5 %copy-start.2 = (f32[1024]{0:T(1024)S(1)}, f32[1024]{0:T(1024)}, u32[]{:S(2)}) copy-start(f32[1024]{0:T(1024)} %get-tuple-element.173) | copy-start | bytes 12292 | tf_op jit(solution)/shard_map/while
  146.2 0.6 copy-start.3
  146.8 6.5 %copy-start.2 = (f32[1024]{0:T(1024)S(1)}, f32[1024]{0:T(1024)}, u32[]{:S(2)}) copy-start(f32[1024]{0:T(1024)} %get-tuple-element.173) | copy-start | bytes 12292 | tf_op jit(solution)/shard_map/while
  153.4 0.6 copy-start.3
  154.0 6.5 %copy-start.2 = (f32[1024]{0:T(1024)S(1)}, f32[1024]{0:T(1024)}, u32[]{:S(2)}) copy-start(f32[1024]{0:T(1024)} %get-tuple-element.173) | copy-start | bytes 12292 | tf_op jit(solution)/shard_map/while
  160.5 0.6 copy-start.3
  161.1 6.5 %copy-start.2 = (f32[1024]{0:T(1024)S(1)}, f32[1024]{0:T(1024)}, u32[]{:S(2)}) copy-start(f32[1024]{0:T(1024)} %get-tuple-element.173) | copy-start | bytes 12292 | tf_op jit(solution)/shard_map/while
  167.7 0.6 copy-start.3
  168.3 6.5 %copy-start.2 = (f32[1024]{0:T(1024)S(1)}, f32[1024]{0:T(1024)}, u32[]{:S(2)}) copy-start(f32[1024]{0:T(1024)} %get-tuple-element.173) | copy-start | bytes 12292 | tf_op jit(solution)/shard_map/while
  174.9 0.6 copy-start.3
  175.5 6.5 %copy-start.2 = (f32[1024]{0:T(1024)S(1)}, f32[1024]{0:T(1024)}, u32[]{:S(2)}) copy-start(f32[1024]{0:T(1024)} %get-tuple-element.173) | copy-start | bytes 12292 | tf_op jit(solution)/shard_map/while
  182.0 0.6 copy-start.3
